TPU v7x, 512 devices: a whole 4x8x8 slice. The times are simulated.
512 devices in a mesh: dom: 32 (over y, x), feat: 16 (over z, core).
Axes of the slice: x: 4, y: 8, z: 8, core: 2. Of those that a mesh axis runs over, the one named last changes fastest.
Arguments:
- features: bfloat16 [128, 524288], P('feat', 'dom'), may hold values from -6 to 6
- seed_rows: int32 [8192], P('dom'), may hold values from 0 to 16383
- want_rows: int32 [32, 32, 128], P('dom'), may hold values from 0 to 16383
- live_counts: int32 [32, 32], P('dom'), may hold values from 1 to 128, as said below
- hop_one: int32 [15, 8192], P(None, 'dom'), may hold values from 0 to 4095, as said below
- hop_two: int32 [10, 15, 8192], P(None, None, 'dom'), may hold values from 0 to 4095, as said below
- w1_self: bfloat16 [256, 128], replicated, may hold values from -0.5 to 0.5
- w1_neigh: bfloat16 [256, 128], replicated, may hold values from -0.5 to 0.5
- b1: float32 [256], P('feat'), may hold values from -4 to 4
- w2_self: bfloat16 [256, 256], P(None, 'feat'), may hold values from -0.375 to 0.375
- w2_neigh: bfloat16 [256, 256], P(None, 'feat'), may hold values from -0.375 to 0.375
- b2: float32 [256], P('feat'), may hold values from -4 to 4
Outputs:
- embed: float32 [256, 8192], P('feat', 'dom')
Inputs may be any that keep to these rules, and one draw needn't show every extreme that they name: `want_rows`: slots at or beyond live_counts[r, o] are ignored. `live_counts`: in every draw a quarter of the owners, every fourth one from a drawn offset, receive all 128 slots from every requester. `hop_one`: each entry is o * 128 + c, a position in the buffer of the requester that holds seed s, with c < live_counts of that requester and owner o. `hop_two`: each entry is o * 128 + c, a position in the buffer of the requester that holds seed s, with c < live_counts of that requester and owner o.
All inputs are finite; a program needn't handle non-finite values.
Results may differ from a plain program's by a relative error of at most 0.00036.
Values may be sent and summed in bfloat16 or wider, within the bound.
A program may use at most 64 MiB of HBM per device.

v0:
```python
import jax
import jax.numpy as jnp
from jax import lax
from jax.sharding import PartitionSpec as P

OUT = 256
FAN1 = 15
FAN2 = 10
CAP = 128


def sent_together(arrays, axis, dim, along):
    widths = [a.shape[along] for a in arrays]
    both = jnp.concatenate(arrays, axis=along)
    filled = lax.all_gather(both, axis, axis=dim, tiled=True)
    return tuple(jnp.split(filled, [sum(widths[:k]) for k in range(1, len(widths))], axis=along))


def cut_along(shard, dim, peers):
    dims = shard.shape
    pieces = shard.reshape(*dims[:dim], peers, dims[dim] // peers, *dims[dim + 1 :])
    return jnp.moveaxis(pieces, dim, 0)


def sum_at_owner(shard, axis, dim):
    pieces = cut_along(shard, dim, lax.axis_size(axis))
    arrived = lax.all_to_all(pieces, axis, split_axis=0, concat_axis=0, tiled=True)
    return arrived.sum(axis=0)


def copy_for_each(shard, axis):
    peers = lax.axis_size(axis)
    return lax.all_to_all(
        jnp.broadcast_to(shard[None], (peers, *shard.shape)), axis, 0, 0, tiled=True
    )


def of_everyone(shard, axis):
    everything = copy_for_each(shard, axis)
    return jnp.sum(everything, axis=0)


def aggregate_counts(fetched, hop_one, hop_two):
    feat_dev, slots = fetched.shape
    width = CAP * 4
    first = hop_one.reshape(1, -1)
    second = hop_two.reshape(FAN2, -1)
    columns = first.shape[1]

    def add_block(blocks, carry):
        start = blocks * width
        piece = lax.dynamic_slice_in_dim(fetched, start, width, 1)
        place = start + lax.broadcasted_iota(jnp.int32, (width, 1), 0)
        pick_one = (first == place).astype(jnp.bfloat16)
        pick_two = jnp.zeros((width, columns), jnp.bfloat16)
        for sample in range(FAN2):
            pick_two = pick_two + (second[sample : sample + 1] == place).astype(jnp.bfloat16)
        own_sum = carry[0] + jnp.dot(piece, pick_one, preferred_element_type=jnp.float32)
        mean_sum = carry[1] + jnp.dot(piece, pick_two, preferred_element_type=jnp.float32)
        return (own_sum, mean_sum)

    zeros = jnp.zeros((feat_dev, columns), jnp.float32)
    own_sum, mean_sum = lax.fori_loop(0, slots // width, add_block, (zeros, zeros))
    return (own_sum.astype(jnp.bfloat16), (mean_sum * (1.0 / FAN2)).astype(jnp.bfloat16))


def per_device(
    features,
    seed_rows,
    want_rows,
    live_counts,
    hop_one,
    hop_two,
    w1_self,
    w1_neigh,
    b1,
    w2_self,
    w2_neigh,
    b2,
):
    feat_dev = features.shape[0]
    seed_dev = seed_rows.shape[0]
    hid_dev = b1.shape[0]
    served = jnp.take(
        features,
        lax.all_to_all(want_rows, "dom", split_axis=1, concat_axis=0, tiled=True)[:, 0, :],
        axis=1,
    )
    returned = lax.all_to_all(served, "dom", split_axis=1, concat_axis=1, tiled=True)
    slot_ids = lax.broadcasted_iota(jnp.int32, (1, returned.shape[2]), 1)
    live_slots = slot_ids < live_counts[0][:, None]
    fetched = jnp.where(live_slots[None], returned, jnp.zeros((), jnp.bfloat16)).reshape(
        feat_dev, -1
    )
    x_one, m_two = aggregate_counts(fetched, hop_one, hop_two)
    x_seed = jnp.take(features, seed_rows, axis=1)
    m_one = jnp.sum(x_one.reshape(feat_dev, FAN1, seed_dev), axis=1, dtype=jnp.float32)
    m_one = (m_one * (1.0 / FAN1)).astype(jnp.bfloat16)
    selves = jnp.concatenate([x_one, x_seed], axis=1)
    means = jnp.concatenate([m_two, m_one], axis=1)
    hid_start = lax.axis_index("feat") * hid_dev
    self_rows = lax.dynamic_slice_in_dim(w1_self, hid_start, hid_dev, 0)
    neigh_rows = lax.dynamic_slice_in_dim(w1_neigh, hid_start, hid_dev, 0)
    pieces = sent_together((selves, means), "feat", 0, 1)
    self_part = self_rows
    neigh_part = neigh_rows
    total = jnp.dot(self_part, pieces[0], preferred_element_type=jnp.float32)
    pre = total + jnp.dot(neigh_part, pieces[1], preferred_element_type=jnp.float32)
    hidden = jnp.maximum(pre + b1[:, None], 0.0)
    hop_cols = FAN1 * seed_dev
    h_one = hidden[:, :hop_cols]
    h_seed = hidden[:, hop_cols:]
    g_mean = jnp.sum(h_one.reshape(hid_dev, FAN1, seed_dev), axis=1) * (1.0 / FAN1)
    second_self = w2_self.astype(jnp.float32)
    second_neigh = w2_neigh.astype(jnp.float32)
    self_part = second_self
    neigh_part = second_neigh
    total = jnp.dot(
        self_part, h_seed, precision=lax.Precision.HIGHEST, preferred_element_type=jnp.float32
    )
    z_out = (
        sum_at_owner(
            total
            + jnp.dot(
                neigh_part,
                g_mean,
                precision=lax.Precision.HIGHEST,
                preferred_element_type=jnp.float32,
            ),
            "feat",
            0,
        )
        + b2[:, None]
    )
    square = of_everyone(jnp.sum(z_out * z_out, axis=0), "feat")
    return z_out * lax.rsqrt(square * (1.0 / OUT) + 1.0)


def solution(mesh):
    return jax.shard_map(
        per_device,
        mesh=mesh,
        in_specs=(
            P("feat", "dom"),
            P("dom"),
            P("dom", None, None),
            P("dom", None),
            P(None, "dom"),
            P(None, None, "dom"),
            P(),
            P(),
            P("feat"),
            P(None, "feat"),
            P(None, "feat"),
            P("feat"),
        ),
        out_specs=P("feat", "dom"),
        check_vma=False,
    )
```

profile of v0, /device:TPU:1, one launch (start us, length us, event | category | flops | bytes accessed | tf_op | source)
XLA Modules:
  0.0 216.7 jit_solution(4721729493136594840)
XLA Ops:
  6.5 0.0 copy-start
  6.5 10.6 %all-to-all-start = ((s32[1,32,128]{2,0,1:T(1,128)}), s32[1,32,128]{2,0,1:T(1,128)S(1)}, u32[]{:S(2)}, u32[]{:S(2)}) async-start(s32[1,32,128]{2,0,1:T(1,128)} %bitcast.37), calls=%async_computation | async-start | bytes 32768 | tf_op jit(solution)/shard_map/all_to_all | solution.py:86
  17.2 0.7 compare_select_fusion.2
  17.9 0.7 compare_and_fusion.1
  18.5 4.0 %copy.32 = bf16[8,16384]{0,1:T(8,128)(2,1)} copy(bf16[8,16384]{1,0:T(8,128)(2,1)} %param.14) | data formatting | bytes 524288 | tf_op args[0]
  22.5 3.5 %gather_fusion.1 = bf16[256,8]{1,0:T(8,128)(2,1)S(1)} fusion(bf16[8,16384]{0,1:T(8,128)(2,1)} %copy.32, s32[1024]{0:T(1024)S(1)} %pad_clamp_fusion), kind=kCustom, calls=%fused_computation.1 | custom fusion | bytes 9216 | tf_op jit(solution)/shard_map/jit(_take)/gather | solution.py:96
  26.0 0.1 select_bitcast_fusion
  26.1 0.0 copy-done.1
  26.1 0.1 copy.39
  26.3 0.0 copy-done.2
  26.3 0.1 copy.35
  26.4 0.0 all-to-all-done
  26.4 13.8 %gather_fusion = bf16[4096,8]{1,0:T(8,128)(2,1)S(1)} fusion(bf16[8,16384]{0,1:T(8,128)(2,1)} %copy.32, s32[4096]{0:T(1024)S(1)} %fusion.38), kind=kCustom, calls=%fused_computation | custom fusion | bytes 147456 | tf_op jit(solution)/shard_map/jit(_take)/gather | solution.py:84
  40.2 0.3 copy.33
  40.6 0.6 select_bitcast_fusion.1
  41.2 9.2 %all-to-all-start.1 = ((bf16[8,32,128]{2,0,1:T(8,128)(2,1)}), bf16[8,32,128]{2,0,1:T(8,128)(2,1)S(1)}, u32[]{:S(2)}, u32[]{:S(2)}) async-start(bf16[8,32,128]{2,0,1:T(8,128)(2,1)} %select_bitcast_fusion.1), calls=%async_computation.1 | async-start | bytes 131072 | tf_op jit(solution)/shard_map/all_to_all | solution.py:89
  50.4 0.2 all-gather.2.cloned.1.call-start
  50.7 0.0 copy-done.7
  50.7 0.1 iota_compare_fusion
  50.7 8.5 %all-to-all-done.1 = bf16[8,32,128]{2,0,1:T(8,128)(2,1)S(1)} async-done(((bf16[8,32,128]{2,0,1:T(8,128)(2,1)}), bf16[8,32,128]{2,0,1:T(8,128)(2,1)S(1)}, u32[]{:S(2)}, u32[]{:S(2)}) %all-to-all-start.1) | async-done | bytes 65568 | tf_op jit(solution)/shard_map/all_to_all | solution.py:89
  59.3 0.0 copy-start.6
  59.3 75.7 %while.16 = (s32[]{:T(128)}, f32[8,3840]{1,0:T(8,128)S(1)}, f32[8,3840]{1,0:T(8,128)S(1)}, bf16[8,4096]{1,0:T(8,128)(2,1)S(1)}, s32[1,3840]{1,0:T(1,128)S(1)}, /...) while((s32[]{:T(128)}, f32[8,3840]{1,0:T(8,128)S(1)}, ...), condition=%wide.region_1.2_spmd.clone, body=%wide.region_0.1_spmd.clone.sunk | while | flops 122020360 | bytes 1032366 | solution.py:63
  59.3 0.4 slice_reduce_fusion.11
  59.7 7.7 %convolution_add_fusion.4 = f32[8,3840]{1,0:T(8,128)S(1)} fusion(s32[3840]{0:T(1024)S(1)} %get-tuple-element.207, s32[3840]{0:T(1024)S(1)} %get-tuple-element.208, s32[3840]{0:T(1024)S(1)} %get-tuple-element.209, s32[3840]{0:T(1024)S(1)} %get-tuple-element.210, s32[3840]{0:T(1024)S(1)} %get-tuple-element.211, s32[3840]{0:T(1024)S(1)} %get-tuple-element.212, ...), kind=kOutput, calls=%fused_computation.14.clone.1 | convolution fusion | flops 88535040 | bytes 419845 | tf_op jit(solution)/shard_map/while/body/eval_jaxpr/dot_general | solution.py:59
  67.4 1.3 fusion.59
  68.8 0.4 slice_reduce_fusion.11
  69.2 7.7 %convolution_add_fusion.4 = f32[8,3840]{1,0:T(8,128)S(1)} fusion(s32[3840]{0:T(1024)S(1)} %get-tuple-element.207, s32[3840]{0:T(1024)S(1)} %get-tuple-element.208, s32[3840]{0:T(1024)S(1)} %get-tuple-element.209, s32[3840]{0:T(1024)S(1)} %get-tuple-element.210, s32[3840]{0:T(1024)S(1)} %get-tuple-element.211, s32[3840]{0:T(1024)S(1)} %get-tuple-element.212, ...), kind=kOutput, calls=%fused_computation.14.clone.1 | convolution fusion | flops 88535040 | bytes 419845 | tf_op jit(solution)/shard_map/while/body/eval_jaxpr/dot_general | solution.py:59
  76.9 1.3 fusion.59
  78.2 0.4 slice_reduce_fusion.11
  78.6 7.7 %convolution_add_fusion.4 = f32[8,3840]{1,0:T(8,128)S(1)} fusion(s32[3840]{0:T(1024)S(1)} %get-tuple-element.207, s32[3840]{0:T(1024)S(1)} %get-tuple-element.208, s32[3840]{0:T(1024)S(1)} %get-tuple-element.209, s32[3840]{0:T(1024)S(1)} %get-tuple-element.210, s32[3840]{0:T(1024)S(1)} %get-tuple-element.211, s32[3840]{0:T(1024)S(1)} %get-tuple-element.212, ...), kind=kOutput, calls=%fused_computation.14.clone.1 | convolution fusion | flops 88535040 | bytes 419845 | tf_op jit(solution)/shard_map/while/body/eval_jaxpr/dot_general | solution.py:59
  86.4 1.3 fusion.59
  87.7 0.4 slice_reduce_fusion.11
  88.1 7.7 %convolution_add_fusion.4 = f32[8,3840]{1,0:T(8,128)S(1)} fusion(s32[3840]{0:T(1024)S(1)} %get-tuple-element.207, s32[3840]{0:T(1024)S(1)} %get-tuple-element.208, s32[3840]{0:T(1024)S(1)} %get-tuple-element.209, s32[3840]{0:T(1024)S(1)} %get-tuple-element.210, s32[3840]{0:T(1024)S(1)} %get-tuple-element.211, s32[3840]{0:T(1024)S(1)} %get-tuple-element.212, ...), kind=kOutput, calls=%fused_computation.14.clone.1 | convolution fusion | flops 88535040 | bytes 419845 | tf_op jit(solution)/shard_map/while/body/eval_jaxpr/dot_general | solution.py:59
  95.8 1.3 fusion.59
  97.2 0.4 slice_reduce_fusion.11
  97.6 7.7 %convolution_add_fusion.4 = f32[8,3840]{1,0:T(8,128)S(1)} fusion(s32[3840]{0:T(1024)S(1)} %get-tuple-element.207, s32[3840]{0:T(1024)S(1)} %get-tuple-element.208, s32[3840]{0:T(1024)S(1)} %get-tuple-element.209, s32[3840]{0:T(1024)S(1)} %get-tuple-element.210, s32[3840]{0:T(1024)S(1)} %get-tuple-element.211, s32[3840]{0:T(1024)S(1)} %get-tuple-element.212, ...), kind=kOutput, calls=%fused_computation.14.clone.1 | convolution fusion | flops 88535040 | bytes 419845 | tf_op jit(solution)/shard_map/while/body/eval_jaxpr/dot_general | solution.py:59
  105.3 1.3 fusion.59
  106.6 0.4 slice_reduce_fusion.11
  107.0 7.7 %convolution_add_fusion.4 = f32[8,3840]{1,0:T(8,128)S(1)} fusion(s32[3840]{0:T(1024)S(1)} %get-tuple-element.207, s32[3840]{0:T(1024)S(1)} %get-tuple-element.208, s32[3840]{0:T(1024)S(1)} %get-tuple-element.209, s32[3840]{0:T(1024)S(1)} %get-tuple-element.210, s32[3840]{0:T(1024)S(1)} %get-tuple-element.211, s32[3840]{0:T(1024)S(1)} %get-tuple-element.212, ...), kind=kOutput, calls=%fused_computation.14.clone.1 | convolution fusion | flops 88535040 | bytes 419845 | tf_op jit(solution)/shard_map/while/body/eval_jaxpr/dot_general | solution.py:59
  114.8 1.3 fusion.59
  116.1 0.4 slice_reduce_fusion.11
  116.5 7.7 %convolution_add_fusion.4 = f32[8,3840]{1,0:T(8,128)S(1)} fusion(s32[3840]{0:T(1024)S(1)} %get-tuple-element.207, s32[3840]{0:T(1024)S(1)} %get-tuple-element.208, s32[3840]{0:T(1024)S(1)} %get-tuple-element.209, s32[3840]{0:T(1024)S(1)} %get-tuple-element.210, s32[3840]{0:T(1024)S(1)} %get-tuple-element.211, s32[3840]{0:T(1024)S(1)} %get-tuple-element.212, ...), kind=kOutput, calls=%fused_computation.14.clone.1 | convolution fusion | flops 88535040 | bytes 419845 | tf_op jit(solution)/shard_map/while/body/eval_jaxpr/dot_general | solution.py:59
  124.2 1.3 fusion.59
  125.6 0.4 slice_reduce_fusion.11
  126.0 7.7 %convolution_add_fusion.4 = f32[8,3840]{1,0:T(8,128)S(1)} fusion(s32[3840]{0:T(1024)S(1)} %get-tuple-element.207, s32[3840]{0:T(1024)S(1)} %get-tuple-element.208, s32[3840]{0:T(1024)S(1)} %get-tuple-element.209, s32[3840]{0:T(1024)S(1)} %get-tuple-element.210, s32[3840]{0:T(1024)S(1)} %get-tuple-element.211, s32[3840]{0:T(1024)S(1)} %get-tuple-element.212, ...), kind=kOutput, calls=%fused_computation.14.clone.1 | convolution fusion | flops 88535040 | bytes 419845 | tf_op jit(solution)/shard_map/while/body/eval_jaxpr/dot_general | solution.py:59
  133.7 1.3 fusion.59
  135.0 0.0 copy-start.5
  135.1 0.7 pad_maximum_fusion
  135.8 0.0 all-gather.2.cloned.1.call-update
  135.8 43.4 %all-gather.2.cloned.1.call-done = bf16[128,8192]{1,0:T(8,128)(2,1)} async-done(((bf16[8,8192]{1,0:T(8,128)(2,1)}), bf16[128,8192]{1,0:T(8,128)(2,1)}) %all-gather.2.cloned.1.call-update) | async-done | bytes 2097168 | tf_op jit(solution)/shard_map/all_gather | solution.py:15
  179.2 0.0 copy-done
  179.2 1.5 fusion.35
  180.7 0.0 copy-done.6
  180.7 1.5 fusion.33
  182.2 0.1 reshape.102
  182.3 0.0 copy-done.4
  182.3 0.3 fusion.39
  182.7 0.0 copy-done.3
  182.7 0.3 convolution_add_fusion.2
  183.0 15.8 %all_to_all.25 = f32[16,16,256]{2,1,0:T(8,128)S(1)} all-to-all(f32[16,16,256]{2,1,0:T(8,128)S(1)} %bitcast.30), channel_id=1, replica_groups=mesh['dom'=32,'feat'=16] {'feat'}, dimensions={0} | all-to-all | bytes 524288 | tf_op jit(solution)/shard_map/all_to_all | solution.py:27
  198.9 0.0 copy-done.5
  198.9 0.1 multiply_reduce_fusion
  199.0 10.1 %all_to_all.26 = f32[16,1,256]{2,1,0:T(1,128)S(1)} all-to-all(f32[16,1,256]{2,1,0:T(1,128)S(1)} %broadcast_in_dim.55), channel_id=1, replica_groups=mesh['dom'=32,'feat'=16] {'feat'}, dimensions={0} | all-to-all | bytes 32768 | tf_op jit(solution)/shard_map/all_to_all | solution.py:33
  209.1 0.7 add_multiply_fusion
  (39 shorter events, 0.6 us)
Async XLA Ops:
  6.5 172.7 %copy-start = (bf16[256,128]{1,0:T(8,128)(2,1)S(1)}, bf16[256,128]{1,0:T(8,128)(2,1)}, u32[]{:S(2)}) copy-start(bf16[256,128]{1,0:T(8,128)(2,1)} %param.20) | copy-start | bytes 196612
  6.5 19.6 %copy-start.1 = (s32[10,15,256]{2,1,0:T(8,128)S(1)}, s32[10,15,256]{2,1,0:T(8,128)}, u32[]{:S(2)}) copy-start(s32[10,15,256]{2,1,0:T(8,128)} %param.19) | copy-start | bytes 460804
  6.5 19.7 %copy-start.2 = (s32[15,256]{1,0:T(8,128)S(1)}, s32[15,256]{1,0:T(8,128)}, u32[]{:S(2)}) copy-start(s32[15,256]{1,0:T(8,128)} %param.18) | copy-start | bytes 46084
  6.5 44.1 %copy-start.7 = (s32[1,32]{1,0:T(1,128)S(1)}, s32[1,32]{1,0:T(1,128)}, u32[]{:S(2)}) copy-start(s32[1,32]{1,0:T(1,128)} %param.17) | copy-start | bytes 388
  6.5 19.8 %all-to-all-start = ((s32[1,32,128]{2,0,1:T(1,128)}), s32[1,32,128]{2,0,1:T(1,128)S(1)}, u32[]{:S(2)}, u32[]{:S(2)}) async-start(s32[1,32,128]{2,0,1:T(1,128)} %bitcast.37), calls=%async_computation | async-start | bytes 32768 | tf_op jit(solution)/shard_map/all_to_all | solution.py:86
  41.2 18.1 %all-to-all-start.1 = ((bf16[8,32,128]{2,0,1:T(8,128)(2,1)}), bf16[8,32,128]{2,0,1:T(8,128)(2,1)S(1)}, u32[]{:S(2)}, u32[]{:S(2)}) async-start(bf16[8,32,128]{2,0,1:T(8,128)(2,1)} %select_bitcast_fusion.1), calls=%async_computation.1 | async-start | bytes 131072 | tf_op jit(solution)/shard_map/all_to_all | solution.py:89
  50.4 128.8 %all-gather.2.cloned.1.call-start = ((), (), s32[]{:S(2)}) async-start(), calls=%async_computation.4 | async-start | bytes 2228224 | tf_op jit(solution)/shard_map/all_gather | solution.py:15
  59.3 121.4 %copy-start.6 = (f32[16]{0:T(128)S(1)}, f32[16]{0:T(128)}, u32[]{:S(2)}) copy-start(f32[16]{0:T(128)} %param.22) | copy-start | bytes 196
  135.0 47.3 %copy-start.4 = (bf16[256,16]{0,1:T(8,128)(2,1)S(1)}, bf16[256,16]{0,1:T(8,128)(2,1)}, u32[]{:S(2)}) copy-start(bf16[256,16]{0,1:T(8,128)(2,1)} %param.23) | copy-start | bytes 24580
  135.0 47.7 %copy-start.3 = (bf16[256,16]{0,1:T(8,128)(2,1)S(1)}, bf16[256,16]{0,1:T(8,128)(2,1)}, u32[]{:S(2)}) copy-start(bf16[256,16]{0,1:T(8,128)(2,1)} %param.24) | copy-start | bytes 24580
  135.0 63.8 %copy-start.5 = (f32[16]{0:T(128)S(1)}, f32[16]{0:T(128)}, u32[]{:S(2)}) copy-start(f32[16]{0:T(128)} %param.25) | copy-start | bytes 196
Sparse Core Ops, SparseCore 0:
  135.9 43.2 all-gather.1
where the time goes:
time: 217 us
  matrix products  75.6 us (35%)
  waiting for transfers between devices  52 us (24%)
  blocking collectives  25.9 us (12%)
  local copies, waits for them, and re-layouts  25 us (12%)
  starting transfers between devices  20.1 us (9%)
  between operations  13.6 us (6%)
  other arithmetic  4.19 us (2%)
    dot_general x8, matrix products, add_block(): jnp.dot(piece, pick_two, preferred_element_type=jnp.float32)  61.3 us
    all_gather x1, waiting for transfers between devices, sent_together(): filled = lax.all_gather(both, axis, axis=dim, tiled=True)  43.4 us
    all_to_all x1, blocking collectives, sum_at_owner(): lax.all_to_all(pieces, axis, split_axis=0, concat_axis=0, tiled=True)  15.8 us
    gather x2, local copies, waits for them, and re-layouts, per_device(): jnp.take(features, lax.all_to_all(want_rows, 'dom', split_axis=1, concat_...  14.1 us
    dot_general x8, matrix products, add_block(): jnp.dot(piece, pick_one, preferred_element_type=jnp.float32)  10.7 us
    all_to_all x1, starting transfers between devices, per_device(): lax.all_to_all(want_rows, 'dom', split_axis=1, concat_axis=0, tiled=True)  10.6 us
    all_to_all x1, blocking collectives, copy_for_each(): lax.all_to_all(jnp.broadcast_to(shard[None], (peers, *shard.shape)), axis...  10.1 us
    all_to_all x1, starting transfers between devices, per_device(): lax.all_to_all(served, 'dom', split_axis=1, concat_axis=1, tiled=True)  9.23 us
  transfers between devices with their start and end apart: 3, of which 2 were waited for; matrix products, arithmetic and copies ran while one was open for 4% of the time, Pallas kernels for 0%

commit v1 on v0

v1 whole, which is shorter than its diff:
```python
import jax
import jax.numpy as jnp
from jax import lax
from jax.experimental import pallas as pl
from jax.experimental.pallas import tpu as pltpu
from jax.sharding import PartitionSpec as P

OUT = 256
FAN1 = 15
FAN2 = 10
CAP = 128
DOM = 32
FEAT_DEV = 16
RING = 8
CHUNKS = 4
PER = DOM // CHUNKS
MESH = pl.DeviceIdType.MESH
BF = jnp.bfloat16
F32 = jnp.float32


def iota(shape, dim):
    return lax.broadcasted_iota(jnp.int32, shape, dim)


def dot(a, b):
    return jnp.dot(a, b, preferred_element_type=F32)


def halves(x):
    high = x.astype(BF)
    return high, (x - high.astype(F32)).astype(BF)


def thirds(x):
    high = x.astype(BF)
    rest = x - high.astype(F32)
    mid = rest.astype(BF)
    return high, mid, (rest - mid.astype(F32)).astype(BF)


def swap_groups(x):
    row, group = iota((8, 128), 0), iota((8, 128), 1) // 16
    for bit in (1, 2, 4):
        down = pltpu.roll(pltpu.roll(x, bit, 0), 128 - 16 * bit, 1)
        up = pltpu.roll(pltpu.roll(x, 8 - bit, 0), 16 * bit, 1)
        low_row, low_group = (row & bit) == 0, (group & bit) == 0
        x = jnp.where(low_row == low_group, x, jnp.where(low_row, up, down))
    return x


def kernel(
    tab_ref, seed_ref, want_ref, live_ref, hop1_ref, hop2_ref, w1s_ref, w1n_ref, b1_ref, w2s_ref, w2n_ref, b2_ref,
    out_ref,
    table, wants, asked, picked, fetched, seeds_own, seeds_all, w2s_all, w2n_all, bias_own, bias_all, counts,
    outgoing, incoming,
    ask_send, ask_recv, pick_send, pick_recv, small_send, small_recv, ring_send, ring_recv, pair_send, pair_recv,
    last_send, last_recv,
):
    me_dom, me = lax.axis_index("dom"), lax.axis_index("feat")
    z, core = me // 2, lax.rem(me, 2)

    def remote(src, dst, send, recv, **where):
        return pltpu.make_async_remote_copy(
            src_ref=src, dst_ref=dst, send_sem=send, recv_sem=recv, device_id=where, device_id_type=MESH
        )

    barrier = pltpu.get_barrier_semaphore()

    def greet(i, _):
        pl.semaphore_signal(barrier, inc=1, device_id={"dom": lax.rem(me_dom + i, DOM)}, device_id_type=MESH)
        return 0

    def greet_feat(i, _):
        pl.semaphore_signal(barrier, inc=1, device_id={"feat": lax.rem(me + i, FEAT_DEV)}, device_id_type=MESH)
        return 0

    lax.fori_loop(1, DOM, greet, 0)
    lax.fori_loop(1, FEAT_DEV, greet_feat, 0)

    eye = iota((DOM, DOM), 0) == iota((DOM, DOM), 1)
    live = jnp.where(eye, jnp.broadcast_to(live_ref[...].astype(F32), (DOM, DOM)), 0.0)
    live = jnp.sum(live, axis=1, keepdims=True).astype(jnp.int32)
    asks = jnp.where(iota((DOM, CAP), 1) < live, want_ref[...], -1)
    wants[...] = asks.reshape(DOM, 1, CAP)

    spot = (iota((16, OUT), 1) == iota((16, OUT), 0) + 16 * me).astype(BF)
    for row, ref in enumerate((b1_ref, b2_ref)):
        placed = sum(dot(part, spot) for part in thirds(jnp.broadcast_to(ref[...], (8, 16))))
        bias_own[row : row + 1, :] = placed[0:1]

    for pair in range(32):
        left = tab_ref[:, pl.ds(512 * pair, 256)]
        right = tab_ref[:, pl.ds(512 * pair + 256, 256)]
        table[pl.ds(16 * pair, 16), :] = jnp.concatenate([left, right], axis=0)

    def pick(rows):
        low = jnp.where(rows >= 0, rows & 255, -1)
        high = jnp.broadcast_to(rows >> 8, (8, 256))
        chosen = (iota((256, 256), 0) == low).astype(BF)
        found = dot(table[...], chosen)
        parts = [found[8 * h : 8 * h + 8] for h in range(64)]
        for bit in range(6):
            upper = (high & (1 << bit)) != 0
            parts = [jnp.where(upper, parts[2 * i + 1], parts[2 * i]) for i in range(len(parts) // 2)]
        return parts[0].astype(BF)

    seeds_own[...] = pick(seed_ref[...])

    pl.semaphore_wait(barrier, DOM - 1 + FEAT_DEV - 1)

    def ask(i, _):
        to = lax.rem(me_dom + i, DOM)
        remote(wants.at[to], asked.at[me_dom], ask_send, ask_recv, dom=to).start()
        return 0

    own_ask = pltpu.make_async_copy(wants.at[me_dom], asked.at[me_dom], ask_recv)
    own_ask.start()
    lax.fori_loop(1, DOM, ask, 0)

    w2_rows = pl.ds(pl.multiple_of(16 * me, 16), 16)
    small = (
        (seeds_own, seeds_all.at[me]),
        (w2s_ref, w2s_all.at[w2_rows, :]),
        (w2n_ref, w2n_all.at[w2_rows, :]),
        (bias_own, bias_all.at[me]),
    )
    for kind, (src, dst) in enumerate(small):
        pltpu.make_async_copy(src, dst, small_recv.at[kind]).start()

    def spread(i, _):
        to = lax.rem(me + i, FEAT_DEV)
        for kind, (src, dst) in enumerate(small):
            remote(src, dst, small_send.at[kind], small_recv.at[kind], feat=to).start()
        return 0

    lax.fori_loop(1, FEAT_DEV, spread, 0)

    mine = (iota((256, 256), 0) == lax.rem(iota((256, 256), 1), 16) + 16 * me).astype(BF)
    keep = iota((FAN1, 256), 1) // 16 == iota((FAN1, 256), 0)

    def row_of(hops):
        high = dot((hops >> 7).astype(F32).astype(BF), mine)
        low = dot((hops & 127).astype(F32).astype(BF), mine)
        place = jnp.sum(jnp.where(keep, high * 128.0 + low, 0.0), axis=0, keepdims=True)
        place = jnp.where(iota((1, 256), 1) < 16 * FAN1, place, -1.0)
        return place.astype(jnp.int32)

    first = row_of(hop1_ref[...])
    second = [row_of(hop2_ref[k]) for k in range(FAN2)]
    first = jnp.broadcast_to(first, (8, 256))
    second = [jnp.broadcast_to(row, (8, 256)) for row in second]

    def count(block, _):
        ones, tens = [], []
        for half in range(2):
            place = iota((8, 256), 0) + (block * 16 + half * 8)
            ones.append((first == place).astype(F32))
            total = (second[0] == place).astype(F32)
            for row in second[1:]:
                total = total + (row == place).astype(F32)
            tens.append(total)
        rows = pl.ds(pl.multiple_of(block * 16, 16), 16)
        counts[rows, 0:256] = jnp.concatenate(ones, axis=0).astype(BF)
        counts[rows, 256:512] = jnp.concatenate(tens, axis=0).astype(BF)
        return 0

    lax.fori_loop(0, DOM * CAP // 16, count, 0)

    pltpu.make_async_copy(wants, asked, ask_recv).wait()

    def chunk_of(owner):
        return owner // PER

    def serve(i, _):
        base = 2 * lax.rem(me_dom // 2 + i, DOM // 2)
        rows = jnp.concatenate([asked[base], asked[base + 1]], axis=1)
        got = pick(rows)
        for half in range(2):
            to = base + half
            picked[to] = got[:, 128 * half : 128 * half + 128]
            mine_too = to == me_dom

            @pl.when(mine_too)
            def _():
                pltpu.make_async_copy(
                    picked.at[to], fetched.at[me_dom, me], pick_recv.at[chunk_of(me_dom)]
                ).start()

            @pl.when(jnp.logical_not(mine_too))
            def _():
                remote(
                    picked.at[to], fetched.at[me_dom, me], pick_send, pick_recv.at[chunk_of(me_dom)], dom=to
                ).start()

        return 0

    lax.fori_loop(0, DOM // 2, serve, 0)

    def owners(q):
        return pl.ds(PER * q, PER)

    def block(q, origin):
        return fetched.at[owners(q), origin]

    up, down = lax.rem(z + 1, RING) * 2 + core, lax.rem(z + RING - 1, RING) * 2 + core
    partner = 2 * z + 1 - core

    def reach(q, way):
        return 4 if (q + way) % 2 == 0 else 3

    def origin_of(way, hop):
        return lax.rem(z + (RING - hop if way == 0 else hop), RING) * 2 + core

    def pass_on(q, way, hop):
        return remote(
            block(q, origin_of(way, hop)),
            block(q, origin_of(way, hop)),
            ring_send.at[way, hop, q],
            ring_recv.at[way, hop, q],
            feat=up if way == 0 else down,
        )

    def to_partner(q, way, hop):
        slot = hop if way == 0 else 4 + hop
        at = block(q, origin_of(way, hop))
        return remote(at, at, pair_send.at[slot, q], pair_recv.at[slot, q], feat=partner)

    started = []

    def go(copy):
        copy.start()
        started.append(copy)

    for q in range(CHUNKS):
        pltpu.make_async_copy(block(q, 0), block(q, 1), pick_recv.at[q]).wait()
        for way in range(2):
            go(pass_on(q, way, 0))
        go(to_partner(q, 0, 0))
    for hop in range(1, 5):
        for q in range(CHUNKS):
            for way in range(2):
                if hop <= reach(q, way):
                    pass_on(q, way, hop - 1).wait_recv()
                    if hop < reach(q, way):
                        go(pass_on(q, way, hop))
                    go(to_partner(q, way, hop))

    total = jnp.zeros((128, 512), F32)
    for q in range(CHUNKS):
        to_partner(q, 0, 0).wait_recv()
        for hop in range(1, 5):
            for way in range(2):
                if hop <= reach(q, way):
                    to_partner(q, way, hop).wait_recv()
        for pair in range(PER // 2):
            o = PER * q + 2 * pair
            left = fetched[o].reshape(128, CAP)
            right = fetched[o + 1].reshape(128, CAP)
            total = total + dot(jnp.concatenate([left, right], axis=1), counts[pl.ds(o * CAP, 256), :])

    for kind, (whole, part) in enumerate(
        ((seeds_all, seeds_all), (w2s_all, w2s_all), (w2n_all, w2n_all), (bias_all, bias_all))
    ):
        pltpu.make_async_copy(whole, part, small_recv.at[kind]).wait()

    seed_lane = iota((256, 256), 1) - 16 * FAN1
    own_seeds = ((iota((256, 256), 0) == seed_lane + 16 * me) & (seed_lane >= 0)).astype(BF)
    selves = (total[:, :256] + dot(seeds_all[...].reshape(128, 256), own_seeds)).T
    sums = total[:, 256:].T
    one_sum = selves[0:16]
    for j in range(1, FAN1):
        one_sum = one_sum + selves[16 * j : 16 * j + 16]
    means = jnp.concatenate([sums[: 16 * FAN1] * (1.0 / FAN2), one_sum * (1.0 / FAN1)], axis=0).astype(BF)
    selves = selves.astype(BF)

    def nt(a, b):
        return lax.dot_general(a, b, (((1,), (1,)), ((), ())), preferred_element_type=F32)

    biases = jnp.sum(bias_all[...], axis=0)
    hidden = nt(selves, w1s_ref[...]) + nt(means, w1n_ref[...])
    hidden = jnp.maximum(hidden + biases[0:1], 0.0)
    g = hidden[0:16]
    for j in range(1, FAN1):
        g = g + hidden[16 * j : 16 * j + 16]
    g = g * (1.0 / FAN1)
    h_seed = hidden[16 * FAN1 :]
    z_out = biases[1:2]
    for part in halves(h_seed):
        z_out = z_out + dot(part, w2s_all[...])
    for part in halves(g):
        z_out = z_out + dot(part, w2n_all[...])
    square = jnp.sum(z_out * z_out, axis=1, keepdims=True)
    embed = z_out * lax.rsqrt(square * (1.0 / OUT) + 1.0)

    for a in range(2):
        for h in range(2):
            turned = swap_groups(embed[8 * a : 8 * a + 8, 128 * h : 128 * h + 128])
            outgoing[8 * h : 8 * h + 8, a, :] = turned

    pltpu.make_async_copy(outgoing.at[me], incoming.at[me], last_recv).start()

    def hand(i, _):
        to = lax.rem(me + i, FEAT_DEV)
        remote(outgoing.at[to], incoming.at[me], last_send, last_recv, feat=to).start()
        return 0

    lax.fori_loop(1, FEAT_DEV, hand, 0)
    pltpu.make_async_copy(outgoing, incoming, last_recv).wait()

    came = incoming[...].reshape(32, 128).T
    widen = (iota((32, 256), 1) // 8 == iota((32, 256), 0)).astype(BF)
    wide = sum(dot(part, widen) for part in thirds(came))
    lane = lax.rem(iota((16, 256), 1), 8)
    result = jnp.zeros((16, 256), F32)
    for b in range(8):
        result = result + jnp.where(lane == b, wide[16 * b : 16 * b + 16], 0.0)
    out_ref[...] = result

    for copy in started:
        copy.wait_send()
    others = pl.ds(0, DOM - 1)
    pltpu.make_async_copy(wants.at[others], wants.at[others], ask_send).wait()
    pltpu.make_async_copy(picked.at[others], picked.at[others], pick_send).wait()
    peers = pl.ds(0, FEAT_DEV - 1)
    rows = pl.ds(0, 16 * (FEAT_DEV - 1))
    pltpu.make_async_copy(seeds_all.at[peers], seeds_all.at[peers], small_send.at[0]).wait()
    pltpu.make_async_copy(w2s_all.at[rows, :], w2s_all.at[rows, :], small_send.at[1]).wait()
    pltpu.make_async_copy(w2n_all.at[rows, :], w2n_all.at[rows, :], small_send.at[2]).wait()
    pltpu.make_async_copy(bias_all.at[peers], bias_all.at[peers], small_send.at[3]).wait()
    pltpu.make_async_copy(outgoing.at[peers], outgoing.at[peers], last_send).wait()


def per_device(
    features, seed_rows, want_rows, live_counts, hop_one, hop_two, w1_self, w1_neigh, b1, w2_self, w2_neigh, b2
):
    vmem = pl.BlockSpec(memory_space=pltpu.VMEM)
    dma = pltpu.SemaphoreType.DMA
    return pl.pallas_call(
        kernel,
        out_shape=jax.ShapeDtypeStruct((16, 256), F32),
        in_specs=[vmem] * 12,
        out_specs=vmem,
        scratch_shapes=[
            pltpu.VMEM((512, 256), BF),
            pltpu.VMEM((DOM, 1, CAP), jnp.int32),
            pltpu.VMEM((DOM, 1, CAP), jnp.int32),
            pltpu.VMEM((DOM, 8, CAP), BF),
            pltpu.VMEM((DOM, FEAT_DEV, 8, CAP), BF),
            pltpu.VMEM((8, 256), BF),
            pltpu.VMEM((FEAT_DEV, 8, 256), BF),
            pltpu.VMEM((256, 256), BF),
            pltpu.VMEM((256, 256), BF),
            pltpu.VMEM((2, 256), F32),
            pltpu.VMEM((FEAT_DEV, 2, 256), F32),
            pltpu.VMEM((DOM * CAP, 512), BF),
            pltpu.VMEM((FEAT_DEV, 2, 128), F32),
            pltpu.VMEM((FEAT_DEV, 2, 128), F32),
            dma, dma, dma, dma((CHUNKS,)), dma((4,)), dma((4,)),
            dma((2, 4, CHUNKS)), dma((2, 4, CHUNKS)), dma((9, CHUNKS)), dma((9, CHUNKS)),
            dma, dma,
        ],
        compiler_params=pltpu.CompilerParams(
            collective_id=0, has_side_effects=True, vmem_limit_bytes=48 * 1024 * 1024
        ),
    )(
        features, seed_rows.reshape(1, -1), want_rows[0], live_counts, hop_one, hop_two, w1_self, w1_neigh,
        b1.reshape(1, -1), w2_self.T, w2_neigh.T, b2.reshape(1, -1),
    )


def solution(mesh):
    return jax.shard_map(
        per_device,
        mesh=mesh,
        in_specs=(
            P("feat", "dom"),
            P("dom"),
            P("dom", None, None),
            P("dom", None),
            P(None, "dom"),
            P(None, None, "dom"),
            P(),
            P(),
            P("feat"),
            P(None, "feat"),
            P(None, "feat"),
            P("feat"),
        ),
        out_specs=P("feat", "dom"),
        check_vma=False,
    )
```

time: 217 us -> 60.6 us (0.28)
  matrix products: 75.6 us -> 0 us
  Pallas kernels: 0 us -> 53.2 us
  waiting for transfers between devices: 52 us -> 0 us
  blocking collectives: 25.9 us -> 0 us
  starting transfers between devices: 20.1 us -> 0 us
  local copies, waits for them, and re-layouts: 25 us -> 6.99 us
  between operations: 13.6 us -> 0.04 us
  other arithmetic: 4.19 us -> 0 us
    dot_general x20 -> x0, matrix products: 75.6 us -> none  [the longest x8 61.3 us: add_block(): jnp.dot(piece, pick_two, preferred_element_type=jnp.float32)]
    pallas_call x0 -> x1, Pallas kernels: none -> 53.2 us  [per_device(): pl.pallas_call(kernel, out_shape=jax.ShapeDtypeStruct((16, 256), F32), in...]
    all_gather x1 -> x0, waiting for transfers between devices: 43.4 us -> none  [sent_together(): filled = lax.all_gather(both, axis, axis=dim, tiled=True)]
    all_to_all x2 -> x0, blocking collectives: 25.9 us -> none  [the longest x1 15.8 us: sum_at_owner(): lax.all_to_all(pieces, axis, split_axis=0, concat_axis=0, tiled=True)]
    all_to_all x2 -> x0, starting transfers between devices: 19.9 us -> none  [the longest x1 10.6 us: per_device(): lax.all_to_all(want_rows, 'dom', split_axis=1, concat_axis=0, tiled=True)]
    gather x3 -> x0, local copies, waits for them, and re-layouts: 17.6 us -> none  [the longest x2 14.1 us: per_device(): jnp.take(features, lax.all_to_all(want_rows, 'dom', split_axis=1, concat_...]
    all_to_all x2 -> x0, waiting for transfers between devices: 8.51 us -> none  [the longest x1 8.51 us: per_device(): lax.all_to_all(served, 'dom', split_axis=1, concat_axis=1, tiled=True)]
    slice x9 -> x0, local copies, waits for them, and re-layouts: 3.13 us -> none  [the longest x8 3.11 us: add_block(): second[sample:sample + 1] == place]
  transfers between devices with their start and end apart: 3 -> 0, of which waited for: 2 -> 0; matrix products, arithmetic and copies ran while one was open for 4% -> 0% of each run, Pallas kernels for 0% -> 0%
where the time goes in v1:
time: 60.6 us; the launch traced here: 60.2 us
  Pallas kernels  53.2 us (88%)
  local copies, waits for them, and re-layouts  6.99 us (12%)
    pallas_call x1, Pallas kernels, per_device(): pl.pallas_call(kernel, out_shape=jax.ShapeDtypeStruct((16, 256), F32), in...  53.2 us
    unnamed x25, local copies, waits for them, and re-layouts  6.99 us

profile of v1, /device:TPU:1, one launch (start us, length us, event | category | flops | bytes accessed | tf_op | source)
XLA Modules:
  0.0 60.2 jit_solution(16288487657987887651)
XLA Ops:
  0.0 0.0 copy-start.6
  0.0 0.0 copy-start.10
  0.0 0.0 copy-start.11
  0.0 0.0 copy-start.8
  0.0 0.0 copy-start.9
  0.0 0.7 %copy-done.6 = bf16[256,16]{0,1:T(8,128)(2,1)S(1)} copy-done((bf16[256,16]{0,1:T(8,128)(2,1)S(1)}, bf16[256,16]{0,1:T(8,128)(2,1)}, u32[]{:S(2)}) %copy-start.6) | copy-done | bytes 8216
  0.7 0.0 copy-done.10
  0.7 0.0 copy-done.11
  0.7 0.0 copy-done.8
  0.7 0.0 copy-done.9
  0.7 0.0 copy-start
  0.7 0.9 %copy-done = bf16[8,16384]{1,0:T(8,128)(2,1)S(1)} copy-done((bf16[8,16384]{1,0:T(8,128)(2,1)S(1)}, bf16[8,16384]{1,0:T(8,128)(2,1)}, u32[]{:S(2)}) %copy-start) | copy-done | bytes 262168
  1.7 0.0 copy-start.1
  1.7 0.9 %copy-done.1 = s32[10,15,256]{2,1,0:T(8,128)S(1)} copy-done((s32[10,15,256]{2,1,0:T(8,128)S(1)}, s32[10,15,256]{2,1,0:T(8,128)}, u32[]{:S(2)}) %copy-start.1) | copy-done | bytes 153624
  2.6 0.0 copy-start.2
  2.6 0.8 %copy-done.2 = bf16[256,128]{1,0:T(8,128)(2,1)S(1)} copy-done((bf16[256,128]{1,0:T(8,128)(2,1)S(1)}, bf16[256,128]{1,0:T(8,128)(2,1)}, u32[]{:S(2)}) %copy-start.2) | copy-done | bytes 65560
  3.4 0.0 copy-start.3
  3.4 0.8 %copy-done.3 = bf16[256,128]{1,0:T(8,128)(2,1)S(1)} copy-done((bf16[256,128]{1,0:T(8,128)(2,1)S(1)}, bf16[256,128]{1,0:T(8,128)(2,1)}, u32[]{:S(2)}) %copy-start.3) | copy-done | bytes 65560
  4.3 0.0 copy-start.4
  4.3 0.7 %copy-done.4 = s32[1,32,128]{2,1,0:T(8,128)S(1)} copy-done((s32[1,32,128]{2,1,0:T(8,128)S(1)}, s32[1,32,128]{2,1,0:T(8,128)}, u32[]{:S(2)}) %copy-start.4) | copy-done | bytes 16408
  5.0 0.0 copy-start.5
  5.0 0.7 %copy-done.5 = s32[15,256]{1,0:T(8,128)S(1)} copy-done((s32[15,256]{1,0:T(8,128)S(1)}, s32[15,256]{1,0:T(8,128)}, u32[]{:S(2)}) %copy-start.5) | copy-done | bytes 15384
  5.7 0.0 copy-start.7
  5.7 0.7 %copy-done.7 = bf16[256,16]{0,1:T(8,128)(2,1)S(1)} copy-done((bf16[256,16]{0,1:T(8,128)(2,1)S(1)}, bf16[256,16]{0,1:T(8,128)(2,1)}, u32[]{:S(2)}) %copy-start.7) | copy-done | bytes 8216
  6.4 53.2 %shard_map.118 = f32[16,256]{1,0:T(8,128)S(1)} custom-call(bf16[8,16384]{1,0:T(8,128)(2,1)S(1)} %copy-done, s32[1,256]{1,0:T(1,128)S(1)} %bitcast.9, s32[32,128]{1,0:T(8,128)S(1)} %bitcast.6, s32[1,32]{1,0:T(1,128)S(1)} %copy-done.9, s32[15,256]{1,0:T(8,128)S(1)} %copy-done.5, s32[10,15,256]{2,1,0:T(8,128)S(1)} %copy-done.1, bf16[256,128]{1,0:T(8,128)(2,1)S(1)} %copy-done.2, ...), custom_call_target="tpu_custom_call" | custom-call | tf_op jit(solution)/shard_map/pallas_call | solution.py:339
  59.6 0.6 %copy.14 = f32[16,256]{1,0:T(8,128)} copy(f32[16,256]{1,0:T(8,128)S(1)} %shard_map.118) | data formatting | bytes 32768
Async XLA Ops:
  0.0 0.7 %copy-start.6 = (bf16[256,16]{0,1:T(8,128)(2,1)S(1)}, bf16[256,16]{0,1:T(8,128)(2,1)}, u32[]{:S(2)}) copy-start(bf16[256,16]{0,1:T(8,128)(2,1)} %param.21) | copy-start | bytes 24580
  0.0 0.7 %copy-start.10 = (f32[16]{0:T(128)S(1)}, f32[16]{0:T(128)}, u32[]{:S(2)}) copy-start(f32[16]{0:T(128)} %param.20) | copy-start | bytes 196
  0.0 0.7 %copy-start.11 = (f32[16]{0:T(128)S(1)}, f32[16]{0:T(128)}, u32[]{:S(2)}) copy-start(f32[16]{0:T(128)} %param.23) | copy-start | bytes 196
  0.0 0.7 %copy-start.8 = (s32[256]{0:T(256)S(1)}, s32[256]{0:T(256)}, u32[]{:S(2)}) copy-start(s32[256]{0:T(256)} %param.13) | copy-start | bytes 3076
  0.0 0.7 %copy-start.9 = (s32[1,32]{1,0:T(1,128)S(1)}, s32[1,32]{1,0:T(1,128)}, u32[]{:S(2)}) copy-start(s32[1,32]{1,0:T(1,128)} %live_ref.1) | copy-start | bytes 388
  0.7 1.0 %copy-start = (bf16[8,16384]{1,0:T(8,128)(2,1)S(1)}, bf16[8,16384]{1,0:T(8,128)(2,1)}, u32[]{:S(2)}) copy-start(bf16[8,16384]{1,0:T(8,128)(2,1)} %tab_ref.1) | copy-start | bytes 786436
  1.7 0.9 %copy-start.1 = (s32[10,15,256]{2,1,0:T(8,128)S(1)}, s32[10,15,256]{2,1,0:T(8,128)}, u32[]{:S(2)}) copy-start(s32[10,15,256]{2,1,0:T(8,128)} %hop2_ref.1) | copy-start | bytes 460804
  2.6 0.8 %copy-start.2 = (bf16[256,128]{1,0:T(8,128)(2,1)S(1)}, bf16[256,128]{1,0:T(8,128)(2,1)}, u32[]{:S(2)}) copy-start(bf16[256,128]{1,0:T(8,128)(2,1)} %w1s_ref.1) | copy-start | bytes 196612
  3.4 0.8 %copy-start.3 = (bf16[256,128]{1,0:T(8,128)(2,1)S(1)}, bf16[256,128]{1,0:T(8,128)(2,1)}, u32[]{:S(2)}) copy-start(bf16[256,128]{1,0:T(8,128)(2,1)} %w1n_ref.1) | copy-start | bytes 196612
  4.3 0.7 %copy-start.4 = (s32[1,32,128]{2,1,0:T(8,128)S(1)}, s32[1,32,128]{2,1,0:T(8,128)}, u32[]{:S(2)}) copy-start(s32[1,32,128]{2,1,0:T(8,128)} %param.14) | copy-start | bytes 49156
  5.0 0.7 %copy-start.5 = (s32[15,256]{1,0:T(8,128)S(1)}, s32[15,256]{1,0:T(8,128)}, u32[]{:S(2)}) copy-start(s32[15,256]{1,0:T(8,128)} %hop1_ref.1) | copy-start | bytes 46084
  5.7 0.7 %copy-start.7 = (bf16[256,16]{0,1:T(8,128)(2,1)S(1)}, bf16[256,16]{0,1:T(8,128)(2,1)}, u32[]{:S(2)}) copy-start(bf16[256,16]{0,1:T(8,128)(2,1)} %param.22) | copy-start | bytes 24580

commit v2 on v1

--- a/solution.py
+++ b/solution.py
@@ -14,6 +14,7 @@
 RING = 8
 CHUNKS = 4
 PER = DOM // CHUNKS
+ORDER = (0, 3, 1, 2)
 MESH = pl.DeviceIdType.MESH
 BF = jnp.bfloat16
 F32 = jnp.float32
@@ -50,12 +51,13 @@
 
 
 def kernel(
-    tab_ref, seed_ref, want_ref, live_ref, hop1_ref, hop2_ref, w1s_ref, w1n_ref, b1_ref, w2s_ref, w2n_ref, b2_ref,
+    tab_in, seed_in, want_in, live_in, hop1_in, hop2_in, w1s_in, w1n_in, b1_in, w2s_in, w2n_in, b2_in,
     out_ref,
+    tab_ref, seed_ref, want_ref, live_ref, hop1_ref, hop2_ref, w1s_ref, w1n_ref, b1_ref, b2_ref,
     table, wants, asked, picked, fetched, seeds_own, seeds_all, w2s_all, w2n_all, bias_own, bias_all, counts,
     outgoing, incoming,
-    ask_send, ask_recv, pick_send, pick_recv, small_send, small_recv, ring_send, ring_recv, pair_send, pair_recv,
-    last_send, last_recv,
+    load_sem, ask_send, ask_recv, pick_send, pick_recv, small_send, small_recv, ring_send, ring_recv, pair_send,
+    pair_recv, last_send, last_recv,
 ):
     me_dom, me = lax.axis_index("dom"), lax.axis_index("feat")
     z, core = me // 2, lax.rem(me, 2)
@@ -75,20 +77,49 @@
         pl.semaphore_signal(barrier, inc=1, device_id={"feat": lax.rem(me + i, FEAT_DEV)}, device_id_type=MESH)
         return 0
 
+    loads = [
+        pltpu.make_async_copy(src, dst, load_sem.at[k])
+        for k, (src, dst) in enumerate(
+            (
+                (want_in, want_ref), (live_in, live_ref), (tab_in, tab_ref), (seed_in, seed_ref), (b1_in, b1_ref),
+                (b2_in, b2_ref), (hop1_in, hop1_ref), (hop2_in, hop2_ref), (w1s_in, w1s_ref), (w1n_in, w1n_ref),
+            )
+        )
+    ]
+    for load in loads:
+        load.start()
     lax.fori_loop(1, DOM, greet, 0)
     lax.fori_loop(1, FEAT_DEV, greet_feat, 0)
 
+    loads[0].wait()
+    loads[1].wait()
     eye = iota((DOM, DOM), 0) == iota((DOM, DOM), 1)
     live = jnp.where(eye, jnp.broadcast_to(live_ref[...].astype(F32), (DOM, DOM)), 0.0)
     live = jnp.sum(live, axis=1, keepdims=True).astype(jnp.int32)
     asks = jnp.where(iota((DOM, CAP), 1) < live, want_ref[...], -1)
     wants[...] = asks.reshape(DOM, 1, CAP)
 
+    loads[4].wait()
+    loads[5].wait()
     spot = (iota((16, OUT), 1) == iota((16, OUT), 0) + 16 * me).astype(BF)
     for row, ref in enumerate((b1_ref, b2_ref)):
         placed = sum(dot(part, spot) for part in thirds(jnp.broadcast_to(ref[...], (8, 16))))
         bias_own[row : row + 1, :] = placed[0:1]
 
+    pl.semaphore_wait(barrier, DOM - 1 + FEAT_DEV - 1)
+
+    own_ask = pltpu.make_async_copy(wants.at[me_dom], asked.at[0], ask_recv.at[0])
+    own_ask.start()
+    for group in ORDER:
+
+        def ask(i, _, group=group):
+            to = lax.rem(me_dom + i, DOM)
+            remote(wants.at[to], asked.at[i], ask_send, ask_recv.at[group], dom=to).start()
+            return 0
+
+        lax.fori_loop(max(1, PER * group), PER * (group + 1), ask, 0)
+
+    loads[2].wait()
     for pair in range(32):
         left = tab_ref[:, pl.ds(512 * pair, 256)]
         right = tab_ref[:, pl.ds(512 * pair + 256, 256)]
@@ -105,24 +136,14 @@
             parts = [jnp.where(upper, parts[2 * i + 1], parts[2 * i]) for i in range(len(parts) // 2)]
         return parts[0].astype(BF)
 
+    loads[3].wait()
     seeds_own[...] = pick(seed_ref[...])
-
-    pl.semaphore_wait(barrier, DOM - 1 + FEAT_DEV - 1)
-
-    def ask(i, _):
-        to = lax.rem(me_dom + i, DOM)
-        remote(wants.at[to], asked.at[me_dom], ask_send, ask_recv, dom=to).start()
-        return 0
-
-    own_ask = pltpu.make_async_copy(wants.at[me_dom], asked.at[me_dom], ask_recv)
-    own_ask.start()
-    lax.fori_loop(1, DOM, ask, 0)
 
     w2_rows = pl.ds(pl.multiple_of(16 * me, 16), 16)
     small = (
         (seeds_own, seeds_all.at[me]),
-        (w2s_ref, w2s_all.at[w2_rows, :]),
-        (w2n_ref, w2n_all.at[w2_rows, :]),
+        (w2s_in, w2s_all.at[w2_rows, :]),
+        (w2n_in, w2n_all.at[w2_rows, :]),
         (bias_own, bias_all.at[me]),
     )
     for kind, (src, dst) in enumerate(small):
@@ -136,133 +157,136 @@
 
     lax.fori_loop(1, FEAT_DEV, spread, 0)
 
+    for k in range(6, 10):
+        loads[k].wait()
     mine = (iota((256, 256), 0) == lax.rem(iota((256, 256), 1), 16) + 16 * me).astype(BF)
     keep = iota((FAN1, 256), 1) // 16 == iota((FAN1, 256), 0)
 
     def row_of(hops):
         high = dot((hops >> 7).astype(F32).astype(BF), mine)
         low = dot((hops & 127).astype(F32).astype(BF), mine)
-        place = jnp.sum(jnp.where(keep, high * 128.0 + low, 0.0), axis=0, keepdims=True)
-        place = jnp.where(iota((1, 256), 1) < 16 * FAN1, place, -1.0)
-        return place.astype(jnp.int32)
+        place = jnp.sum(jnp.where(keep, high * 128.0 + low, 0.0), axis=0, keepdims=True).astype(jnp.int32)
+        place = (place - me_dom * CAP) & (DOM * CAP - 1)
+        place = jnp.where(iota((1, 256), 1) < 16 * FAN1, place, -1)
+        return jnp.broadcast_to(place, (16, 256)).astype(jnp.int16)
 
     first = row_of(hop1_ref[...])
     second = [row_of(hop2_ref[k]) for k in range(FAN2)]
-    first = jnp.broadcast_to(first, (8, 256))
-    second = [jnp.broadcast_to(row, (8, 256)) for row in second]
+
+    one, zero = jnp.ones((16, 256), BF), jnp.zeros((16, 256), BF)
 
     def count(block, _):
-        ones, tens = [], []
+        place = (iota((16, 256), 0) + block * 16).astype(jnp.int16)
+        total = jnp.where(second[0] == place, one, zero)
+        for row in second[1:]:
+            total = total + jnp.where(row == place, one, zero)
+        rows = pl.ds(pl.multiple_of(block * 16, 16), 16)
+        counts[rows, 0:256] = jnp.where(first == place, one, zero)
+        counts[rows, 256:512] = total
+        return 0
+
+    lax.fori_loop(0, DOM * CAP // 16, count, 0)
+
+    def serve_pair(i, local):
+        slot = 2 * i
+        got = pick(jnp.concatenate([asked[slot], asked[slot + 1]], axis=1))
         for half in range(2):
-            place = iota((8, 256), 0) + (block * 16 + half * 8)
-            ones.append((first == place).astype(F32))
-            total = (second[0] == place).astype(F32)
-            for row in second[1:]:
-                total = total + (row == place).astype(F32)
-            tens.append(total)
-        rows = pl.ds(pl.multiple_of(block * 16, 16), 16)
-        counts[rows, 0:256] = jnp.concatenate(ones, axis=0).astype(BF)
-        counts[rows, 256:512] = jnp.concatenate(tens, axis=0).astype(BF)
-        return 0
-
-    lax.fori_loop(0, DOM * CAP // 16, count, 0)
-
-    pltpu.make_async_copy(wants, asked, ask_recv).wait()
-
-    def chunk_of(owner):
-        return owner // PER
-
-    def serve(i, _):
-        base = 2 * lax.rem(me_dom // 2 + i, DOM // 2)
-        rows = jnp.concatenate([asked[base], asked[base + 1]], axis=1)
-        got = pick(rows)
-        for half in range(2):
-            to = base + half
-            picked[to] = got[:, 128 * half : 128 * half + 128]
-            mine_too = to == me_dom
-
-            @pl.when(mine_too)
-            def _():
-                pltpu.make_async_copy(
-                    picked.at[to], fetched.at[me_dom, me], pick_recv.at[chunk_of(me_dom)]
-                ).start()
-
-            @pl.when(jnp.logical_not(mine_too))
-            def _():
-                remote(
-                    picked.at[to], fetched.at[me_dom, me], pick_send, pick_recv.at[chunk_of(me_dom)], dom=to
-                ).start()
-
-        return 0
-
-    lax.fori_loop(0, DOM // 2, serve, 0)
+            picked[slot + half] = got[:, 128 * half : 128 * half + 128]
+            recv = pick_recv.at[slot // PER]
+            if local and half == 0:
+                pltpu.make_async_copy(picked.at[slot], fetched.at[slot, me], recv).start()
+            else:
+                to = lax.rem(me_dom + DOM - slot - half, DOM)
+                remote(picked.at[slot + half], fetched.at[slot + half, me], pick_send, recv, dom=to).start()
+        return 0
 
     def owners(q):
         return pl.ds(PER * q, PER)
 
-    def block(q, origin):
-        return fetched.at[owners(q), origin]
-
-    up, down = lax.rem(z + 1, RING) * 2 + core, lax.rem(z + RING - 1, RING) * 2 + core
+    for group in ORDER:
+        pltpu.make_async_copy(asked.at[owners(group)], asked.at[owners(group)], ask_recv.at[group]).wait()
+        start = PER // 2 * group
+        if group == 0:
+            serve_pair(0, True)
+            start += 1
+        lax.fori_loop(start, PER // 2 * (group + 1), lambda i, _: serve_pair(i, False), 0)
+
+    def block(q, away):
+        return fetched.at[owners(q), lax.rem(z + RING + away, RING) * 2 + core]
+
     partner = 2 * z + 1 - core
-
-    def reach(q, way):
-        return 4 if (q + way) % 2 == 0 else 3
-
-    def origin_of(way, hop):
-        return lax.rem(z + (RING - hop if way == 0 else hop), RING) * 2 + core
-
-    def pass_on(q, way, hop):
-        return remote(
-            block(q, origin_of(way, hop)),
-            block(q, origin_of(way, hop)),
-            ring_send.at[way, hop, q],
-            ring_recv.at[way, hop, q],
-            feat=up if way == 0 else down,
-        )
-
-    def to_partner(q, way, hop):
-        slot = hop if way == 0 else 4 + hop
-        at = block(q, origin_of(way, hop))
-        return remote(at, at, pair_send.at[slot, q], pair_recv.at[slot, q], feat=partner)
-
     started = []
 
     def go(copy):
         copy.start()
         started.append(copy)
 
-    for q in range(CHUNKS):
+    CAME = {0: (-1, -1), 1: (1, 1), 2: (-2, -2), 3: (2, 2), 4: (-3, -1), 5: (3, 1)}
+
+    def flow(kind, q):
+        if kind == 6:
+            away, by = (4, -2) if q % 2 == 0 else (4, 2)
+        else:
+            away, by = CAME[kind]
+        at = block(q, away - by)
+        to = lax.rem(z + RING - by, RING) * 2 + core
+        return remote(at, at, ring_send.at[kind, q], ring_recv.at[kind, q], feat=to)
+
+    def arrival(kind, q):
+        away = 4 if kind == 6 else CAME[kind][0]
+        at = block(q, away)
+        return remote(at, at, ring_send.at[kind, q], ring_recv.at[kind, q], feat=partner)
+
+    def to_partner(kind, q):
+        away = 0 if kind == 7 else 4 if kind == 6 else CAME[kind][0]
+        at = block(q, away)
+        return remote(at, at, pair_send.at[kind, q], pair_recv.at[kind, q], feat=partner)
+
+    def begin(q):
         pltpu.make_async_copy(block(q, 0), block(q, 1), pick_recv.at[q]).wait()
-        for way in range(2):
-            go(pass_on(q, way, 0))
-        go(to_partner(q, 0, 0))
-    for hop in range(1, 5):
-        for q in range(CHUNKS):
-            for way in range(2):
-                if hop <= reach(q, way):
-                    pass_on(q, way, hop - 1).wait_recv()
-                    if hop < reach(q, way):
-                        go(pass_on(q, way, hop))
-                    go(to_partner(q, way, hop))
+        for kind in (2, 3, 0, 1):
+            go(flow(kind, q))
+        go(to_partner(7, q))
+
+    def relay(q):
+        for kind in (2, 3):
+            arrival(kind, q).wait_recv()
+            go(flow(kind + 2, q))
+            if q % 2 == kind % 2:
+                go(flow(6, q))
+            go(to_partner(kind, q))
+
+    def finish(q):
+        for kind in (0, 1, 4, 5, 6):
+            arrival(kind, q).wait_recv()
+            go(to_partner(kind, q))
+
+    a, b, c, d = ORDER
+    begin(a)
+    begin(b)
+    relay(a)
+    relay(b)
+    begin(c)
+    begin(d)
+    finish(a)
+    finish(b)
+    relay(c)
+    relay(d)
+    finish(c)
+    finish(d)
 
     total = jnp.zeros((128, 512), F32)
-    for q in range(CHUNKS):
-        to_partner(q, 0, 0).wait_recv()
-        for hop in range(1, 5):
-            for way in range(2):
-                if hop <= reach(q, way):
-                    to_partner(q, way, hop).wait_recv()
+    for q in ORDER:
+        for kind in range(8):
+            to_partner(kind, q).wait_recv()
         for pair in range(PER // 2):
             o = PER * q + 2 * pair
             left = fetched[o].reshape(128, CAP)
             right = fetched[o + 1].reshape(128, CAP)
             total = total + dot(jnp.concatenate([left, right], axis=1), counts[pl.ds(o * CAP, 256), :])
 
-    for kind, (whole, part) in enumerate(
-        ((seeds_all, seeds_all), (w2s_all, w2s_all), (w2n_all, w2n_all), (bias_all, bias_all))
-    ):
-        pltpu.make_async_copy(whole, part, small_recv.at[kind]).wait()
+    for kind, whole in enumerate((seeds_all, w2s_all, w2n_all, bias_all)):
+        pltpu.make_async_copy(whole, whole, small_recv.at[kind]).wait()
 
     seed_lane = iota((256, 256), 1) - 16 * FAN1
     own_seeds = ((iota((256, 256), 0) == seed_lane + 16 * me) & (seed_lane >= 0)).astype(BF)
@@ -334,14 +358,19 @@
 def per_device(
     features, seed_rows, want_rows, live_counts, hop_one, hop_two, w1_self, w1_neigh, b1, w2_self, w2_neigh, b2
 ):
-    vmem = pl.BlockSpec(memory_space=pltpu.VMEM)
+    hbm = pl.BlockSpec(memory_space=pltpu.HBM)
     dma = pltpu.SemaphoreType.DMA
+    args = (
+        features, seed_rows.reshape(1, -1), want_rows[0], live_counts, hop_one, hop_two, w1_self, w1_neigh,
+        b1.reshape(1, -1), w2_self.T, w2_neigh.T, b2.reshape(1, -1),
+    )
     return pl.pallas_call(
         kernel,
         out_shape=jax.ShapeDtypeStruct((16, 256), F32),
-        in_specs=[vmem] * 12,
-        out_specs=vmem,
+        in_specs=[hbm] * 12,
+        out_specs=pl.BlockSpec(memory_space=pltpu.VMEM),
         scratch_shapes=[
+            *(pltpu.VMEM(args[k].shape, args[k].dtype) for k in (0, 1, 2, 3, 4, 5, 6, 7, 8, 11)),
             pltpu.VMEM((512, 256), BF),
             pltpu.VMEM((DOM, 1, CAP), jnp.int32),
             pltpu.VMEM((DOM, 1, CAP), jnp.int32),
@@ -356,17 +385,13 @@
             pltpu.VMEM((DOM * CAP, 512), BF),
             pltpu.VMEM((FEAT_DEV, 2, 128), F32),
             pltpu.VMEM((FEAT_DEV, 2, 128), F32),
-            dma, dma, dma, dma((CHUNKS,)), dma((4,)), dma((4,)),
-            dma((2, 4, CHUNKS)), dma((2, 4, CHUNKS)), dma((9, CHUNKS)), dma((9, CHUNKS)),
-            dma, dma,
+            dma((10,)), dma, dma((CHUNKS,)), dma, dma((CHUNKS,)), dma((4,)), dma((4,)),
+            dma((7, CHUNKS)), dma((7, CHUNKS)), dma((8, CHUNKS)), dma((8, CHUNKS)), dma, dma,
         ],
         compiler_params=pltpu.CompilerParams(
-            collective_id=0, has_side_effects=True, vmem_limit_bytes=48 * 1024 * 1024
+            collective_id=0, has_side_effects=True, vmem_limit_bytes=60 * 1024 * 1024
         ),
-    )(
-        features, seed_rows.reshape(1, -1), want_rows[0], live_counts, hop_one, hop_two, w1_self, w1_neigh,
-        b1.reshape(1, -1), w2_self.T, w2_neigh.T, b2.reshape(1, -1),
-    )
+    )(*args)
 
 
 def solution(mesh):

time: 60.6 us -> 50.8 us (0.84)
  local copies, waits for them, and re-layouts: 6.99 us -> 1.32 us
  Pallas kernels: 53.2 us -> 49.2 us
    unnamed x25 -> x1, local copies, waits for them, and re-layouts: 6.99 us -> 1.32 us
    pallas_call x1, Pallas kernels: 53.2 us -> 49.2 us  [per_device(): pl.pallas_call(kernel, out_shape=jax.ShapeDtypeStruct((16, 256), F32), in...]
where the time goes in v2:
time: 50.8 us; the launch traced here: 50.5 us
  Pallas kernels  49.2 us (97%)
  local copies, waits for them, and re-layouts  1.32 us (3%)
    pallas_call x1, Pallas kernels, per_device(): pl.pallas_call(kernel, out_shape=jax.ShapeDtypeStruct((16, 256), F32), in...  49.2 us
    unnamed x1, local copies, waits for them, and re-layouts  1.32 us

profile of v2, /device:TPU:1, one launch (start us, length us, event | category | flops | bytes accessed | tf_op | source)
XLA Modules:
  0.0 50.5 jit_solution(2706962455606412192)
XLA Ops:
  0.0 49.2 %shard_map.118 = f32[16,256]{1,0:T(8,128)} custom-call(bf16[8,16384]{1,0:T(8,128)(2,1)} %tab_in.1, s32[1,256]{1,0:T(1,128)} %bitcast.9, s32[32,128]{1,0:T(8,128)} %bitcast.6, s32[1,32]{1,0:T(1,128)} %live_in.1, s32[15,256]{1,0:T(8,128)} %hop1_in.1, s32[10,15,256]{2,1,0:T(8,128)} %hop2_in.1, bf16[256,128]{1,0:T(8,128)(2,1)} %w1s_in.1, ...), custom_call_target="tpu_custom_call" | custom-call | tf_op jit(solution)/shard_map/pallas_call | solution.py:367
  49.2 1.3 %copy.14 = f32[16,256]{1,0:T(8,128)} copy(f32[16,256]{1,0:T(8,128)} %shard_map.118) | data formatting | bytes 32768

commit v3 on v2

--- a/solution.py
+++ b/solution.py
@@ -12,9 +12,13 @@
 DOM = 32
 FEAT_DEV = 16
 RING = 8
-CHUNKS = 4
+CHUNKS = 8
 PER = DOM // CHUNKS
-ORDER = (0, 3, 1, 2)
+ORDER = (0, 7, 1, 6, 2, 5, 3, 4)
+RELAY, DIRECT = 0, 1
+MODE = dict(zip(ORDER, (0, 0, 0, 0, 0, 1, 1, 1)))
+AWAY = (-1, 1, -2, 2, -3, 3, 4)
+LAG = 4
 MESH = pl.DeviceIdType.MESH
 BF = jnp.bfloat16
 F32 = jnp.float32
@@ -69,13 +73,8 @@
 
     barrier = pltpu.get_barrier_semaphore()
 
-    def greet(i, _):
-        pl.semaphore_signal(barrier, inc=1, device_id={"dom": lax.rem(me_dom + i, DOM)}, device_id_type=MESH)
-        return 0
-
-    def greet_feat(i, _):
-        pl.semaphore_signal(barrier, inc=1, device_id={"feat": lax.rem(me + i, FEAT_DEV)}, device_id_type=MESH)
-        return 0
+    def greet(**where):
+        pl.semaphore_signal(barrier, inc=1, device_id=where, device_id_type=MESH)
 
     loads = [
         pltpu.make_async_copy(src, dst, load_sem.at[k])
@@ -88,8 +87,10 @@
     ]
     for load in loads:
         load.start()
-    lax.fori_loop(1, DOM, greet, 0)
-    lax.fori_loop(1, FEAT_DEV, greet_feat, 0)
+    for i in sorted(range(1, DOM), key=lambda i: -min(i, DOM - i)):
+        greet(dom=lax.rem(me_dom + i, DOM))
+    for i in sorted(range(1, FEAT_DEV), key=lambda i: -min(i, FEAT_DEV - i)):
+        greet(feat=lax.rem(me + i, FEAT_DEV))
 
     loads[0].wait()
     loads[1].wait()
@@ -127,8 +128,9 @@
 
     def pick(rows):
         low = jnp.where(rows >= 0, rows & 255, -1)
-        high = jnp.broadcast_to(rows >> 8, (8, 256))
-        chosen = (iota((256, 256), 0) == low).astype(BF)
+        wide = rows.shape[1]
+        high = jnp.broadcast_to(rows >> 8, (8, wide))
+        chosen = (iota((256, wide), 0) == low).astype(BF)
         found = dot(table[...], chosen)
         parts = [found[8 * h : 8 * h + 8] for h in range(64)]
         for bit in range(6):
@@ -175,41 +177,45 @@
 
     one, zero = jnp.ones((16, 256), BF), jnp.zeros((16, 256), BF)
 
-    def count(block, _):
-        place = (iota((16, 256), 0) + block * 16).astype(jnp.int16)
-        total = jnp.where(second[0] == place, one, zero)
-        for row in second[1:]:
-            total = total + jnp.where(row == place, one, zero)
-        rows = pl.ds(pl.multiple_of(block * 16, 16), 16)
-        counts[rows, 0:256] = jnp.where(first == place, one, zero)
-        counts[rows, 256:512] = total
+    def count(owner, _):
+        for part in range(CAP // 16):
+            base = owner * CAP + part * 16
+            place = (iota((16, 256), 0) + base).astype(jnp.int16)
+            total = jnp.where(second[0] == place, one, zero)
+            for row in second[1:]:
+                total = total + jnp.where(row == place, one, zero)
+            rows = pl.ds(pl.multiple_of(base, 16), 16)
+            counts[rows, 0:256] = jnp.where(first == place, one, zero)
+            counts[rows, 256:512] = total
         return 0
 
-    lax.fori_loop(0, DOM * CAP // 16, count, 0)
-
-    def serve_pair(i, local):
-        slot = 2 * i
-        got = pick(jnp.concatenate([asked[slot], asked[slot + 1]], axis=1))
-        for half in range(2):
-            picked[slot + half] = got[:, 128 * half : 128 * half + 128]
-            recv = pick_recv.at[slot // PER]
-            if local and half == 0:
-                pltpu.make_async_copy(picked.at[slot], fetched.at[slot, me], recv).start()
-            else:
-                to = lax.rem(me_dom + DOM - slot - half, DOM)
-                remote(picked.at[slot + half], fetched.at[slot + half, me], pick_send, recv, dom=to).start()
-        return 0
+    counted = [0]
+
+    def count_some(n):
+        lax.fori_loop(counted[0], counted[0] + n, count, 0)
+        counted[0] += n
 
     def owners(q):
         return pl.ds(PER * q, PER)
 
-    for group in ORDER:
+    def serve(group):
         pltpu.make_async_copy(asked.at[owners(group)], asked.at[owners(group)], ask_recv.at[group]).wait()
-        start = PER // 2 * group
-        if group == 0:
-            serve_pair(0, True)
-            start += 1
-        lax.fori_loop(start, PER // 2 * (group + 1), lambda i, _: serve_pair(i, False), 0)
+        slots = range(PER * group, PER * (group + 1))
+        got = pick(jnp.concatenate([asked[slot] for slot in slots], axis=1))
+        for k, slot in enumerate(slots):
+            picked[slot] = got[:, CAP * k : CAP * (k + 1)]
+        for slot in slots:
+            to = lax.rem(me_dom + DOM - slot, DOM)
+            if slot == 0:
+                pltpu.make_async_copy(picked.at[slot], fetched.at[slot, me], pick_recv.at[group]).start()
+            else:
+                remote(picked.at[slot], fetched.at[slot, me], pick_send, pick_recv.at[group], dom=to).start()
+
+    count_some(DOM)
+    for group in ORDER[:4]:
+        serve(group)
+    for group in ORDER[4:]:
+        serve(group)
 
     def block(q, away):
         return fetched.at[owners(q), lax.rem(z + RING + away, RING) * 2 + core]
@@ -221,30 +227,28 @@
         copy.start()
         started.append(copy)
 
-    CAME = {0: (-1, -1), 1: (1, 1), 2: (-2, -2), 3: (2, 2), 4: (-3, -1), 5: (3, 1)}
+    def source(kind, q):
+        if MODE[q] != RELAY or kind < 4:
+            return AWAY[kind]
+        return {4: -1, 5: 1, 6: -2 if ORDER.index(q) % 2 == 0 else 2}[kind]
 
     def flow(kind, q):
-        if kind == 6:
-            away, by = (4, -2) if q % 2 == 0 else (4, 2)
-        else:
-            away, by = CAME[kind]
-        at = block(q, away - by)
+        by = source(kind, q)
+        at = block(q, AWAY[kind] - by)
         to = lax.rem(z + RING - by, RING) * 2 + core
         return remote(at, at, ring_send.at[kind, q], ring_recv.at[kind, q], feat=to)
 
     def arrival(kind, q):
-        away = 4 if kind == 6 else CAME[kind][0]
-        at = block(q, away)
+        at = block(q, AWAY[kind])
         return remote(at, at, ring_send.at[kind, q], ring_recv.at[kind, q], feat=partner)
 
     def to_partner(kind, q):
-        away = 0 if kind == 7 else 4 if kind == 6 else CAME[kind][0]
-        at = block(q, away)
+        at = block(q, 0 if kind == 7 else AWAY[kind])
         return remote(at, at, pair_send.at[kind, q], pair_recv.at[kind, q], feat=partner)
 
     def begin(q):
         pltpu.make_async_copy(block(q, 0), block(q, 1), pick_recv.at[q]).wait()
-        for kind in (2, 3, 0, 1):
+        for kind in {RELAY: (2, 3, 0, 1), DIRECT: (6, 4, 5, 2, 3, 0, 1)}[MODE[q]]:
             go(flow(kind, q))
         go(to_partner(7, q))
 
@@ -252,28 +256,23 @@
         for kind in (2, 3):
             arrival(kind, q).wait_recv()
             go(flow(kind + 2, q))
-            if q % 2 == kind % 2:
+            if source(6, q) == AWAY[kind]:
                 go(flow(6, q))
             go(to_partner(kind, q))
 
     def finish(q):
-        for kind in (0, 1, 4, 5, 6):
+        for kind in (0, 1, 4, 5, 6) if MODE[q] == RELAY else (0, 1, 2, 3, 4, 5, 6):
             arrival(kind, q).wait_recv()
             go(to_partner(kind, q))
 
-    a, b, c, d = ORDER
-    begin(a)
-    begin(b)
-    relay(a)
-    relay(b)
-    begin(c)
-    begin(d)
-    finish(a)
-    finish(b)
-    relay(c)
-    relay(d)
-    finish(c)
-    finish(d)
+    relays = [q for q in ORDER if MODE[q] == RELAY]
+    for step in range(8 + LAG):
+        if step < 8:
+            begin(ORDER[step])
+        if LAG <= step < LAG + len(relays):
+            relay(relays[step - LAG])
+    for step, q in enumerate(ORDER):
+        finish(q)
 
     total = jnp.zeros((128, 512), F32)
     for q in ORDER:
@@ -330,17 +329,6 @@
         return 0
 
     lax.fori_loop(1, FEAT_DEV, hand, 0)
-    pltpu.make_async_copy(outgoing, incoming, last_recv).wait()
-
-    came = incoming[...].reshape(32, 128).T
-    widen = (iota((32, 256), 1) // 8 == iota((32, 256), 0)).astype(BF)
-    wide = sum(dot(part, widen) for part in thirds(came))
-    lane = lax.rem(iota((16, 256), 1), 8)
-    result = jnp.zeros((16, 256), F32)
-    for b in range(8):
-        result = result + jnp.where(lane == b, wide[16 * b : 16 * b + 16], 0.0)
-    out_ref[...] = result
-
     for copy in started:
         copy.wait_send()
     others = pl.ds(0, DOM - 1)
@@ -352,6 +340,17 @@
     pltpu.make_async_copy(w2s_all.at[rows, :], w2s_all.at[rows, :], small_send.at[1]).wait()
     pltpu.make_async_copy(w2n_all.at[rows, :], w2n_all.at[rows, :], small_send.at[2]).wait()
     pltpu.make_async_copy(bias_all.at[peers], bias_all.at[peers], small_send.at[3]).wait()
+
+    pltpu.make_async_copy(outgoing, incoming, last_recv).wait()
+
+    came = incoming[...].reshape(32, 128).T
+    widen = (iota((32, 256), 1) // 8 == iota((32, 256), 0)).astype(BF)
+    wide = sum(dot(part, widen) for part in thirds(came))
+    lane = lax.rem(iota((16, 256), 1), 8)
+    result = jnp.zeros((16, 256), F32)
+    for b in range(8):
+        result = result + jnp.where(lane == b, wide[16 * b : 16 * b + 16], 0.0)
+    out_ref[...] = result
     pltpu.make_async_copy(outgoing.at[peers], outgoing.at[peers], last_send).wait()
 
 

time: 50.8 us -> 48.1 us (0.947)
  Pallas kernels: 49.2 us -> 46.5 us
    pallas_call x1, Pallas kernels: 49.2 us -> 46.5 us  [per_device(): pl.pallas_call(kernel, out_shape=jax.ShapeDtypeStruct((16, 256), F32), in...]
where the time goes in v3:
time: 48.1 us; the launch traced here: 47.8 us
  Pallas kernels  46.5 us (97%)
  local copies, waits for them, and re-layouts  1.32 us (3%)
    pallas_call x1, Pallas kernels, per_device(): pl.pallas_call(kernel, out_shape=jax.ShapeDtypeStruct((16, 256), F32), in...  46.5 us
    unnamed x1, local copies, waits for them, and re-layouts  1.32 us

profile of v3, /device:TPU:1, one launch (start us, length us, event | category | flops | bytes accessed | tf_op | source)
XLA Modules:
  0.0 47.8 jit_solution(18091152358038147597)
XLA Ops:
  0.0 46.5 %shard_map.118 = f32[16,256]{1,0:T(8,128)} custom-call(bf16[8,16384]{1,0:T(8,128)(2,1)} %tab_in.1, s32[1,256]{1,0:T(1,128)} %bitcast.9, s32[32,128]{1,0:T(8,128)} %bitcast.6, s32[1,32]{1,0:T(1,128)} %live_in.1, s32[15,256]{1,0:T(8,128)} %hop1_in.1, s32[10,15,256]{2,1,0:T(8,128)} %hop2_in.1, bf16[256,128]{1,0:T(8,128)(2,1)} %w1s_in.1, ...), custom_call_target="tpu_custom_call" | custom-call | tf_op jit(solution)/shard_map/pallas_call | solution.py:366
  46.5 1.3 %copy.14 = f32[16,256]{1,0:T(8,128)} copy(f32[16,256]{1,0:T(8,128)} %shard_map.118) | data formatting | bytes 32768
